TPU v7x, 128 devices: a whole 4x4x4 slice. The times are simulated.
128 devices in a mesh: row: 8 (over x, core), col: 16 (over y, z).
Axes of the slice: x: 4, y: 4, z: 4, core: 2. Of those that a mesh axis runs over, the one named last changes fastest.
Arguments:
- tokens: bfloat16 [65536, 1024], P(('row', 'col')), may hold values from -6 to 6
- expert_ids: int32 [65536, 1], P(('row', 'col')), may hold values from 0 to 127; in each aligned block of 512 rows (0 to 511, 512 to 1023, ...) at most 8 rows name the same one
- gate_prob: float32 [65536], P(('row', 'col')), may hold values from 0.25 to 1
- norm_gain: float32 [1024], replicated, may hold values from 0.1 to 1.9
- weight_in: bfloat16 [128, 1024, 4096], P(('row', 'col')), may hold values from -0.1875 to 0.1875
- weight_out: bfloat16 [128, 4096, 1024], P(('row', 'col')), may hold values from -0.09375 to 0.09375
Outputs:
- mixed: bfloat16 [65536, 1024], P(('row', 'col'))
- routed: int32 [128], P(('row', 'col'))
Inputs may be any that keep to these rules, and one draw needn't show every extreme that they name: `expert_ids`: among the 512 tokens of one device no expert is chosen more than 8 times; some expert is chosen exactly 8 times by some device's tokens.
All inputs are finite; a program needn't handle non-finite values.
Results may differ from a plain program's by a relative error of at most 0.001.
The roundings to bfloat16 on the way count: a program that leaves them out, or rounds other values in their place, can miss the bound.
Values may be sent and summed in bfloat16 or wider, within the bound.
No kernel may reach another device: no remote copies, remote signals or barrier semaphores. Data moves between devices by JAX's collectives and lax.ppermute only.
A program may use at most 64 MiB of HBM per device.

v0:
```python
import jax
import jax.numpy as jnp
from jax import lax
from jax.sharding import Mesh
from jax.sharding import PartitionSpec as P

ROW = ("row_0", "row_1")
COL = ("col_0", "col_1")
ROW_COL = ("row_0", "row_1", "col_0", "col_1")


def split_up(array, dim, peers):
    before, after = (array.shape[:dim], array.shape[dim + 1 :])
    return jnp.moveaxis(array.reshape(*before, peers, -1, *after), dim, 0)


def sent_and_summed(array, axis, dim):
    parts = split_up(array, dim, lax.axis_size(axis))
    arrived = lax.all_to_all(parts, axis, split_axis=0, concat_axis=0, tiled=True)
    return arrived.sum(axis=0)


def sum_in_two_steps(array, axes, dim):
    far, near = axes
    own = sent_and_summed(split_up(array, dim, lax.axis_size(far)), near, dim + 1)
    return jnp.sum(lax.all_to_all(own, far, 0, 0, tiled=True), axis=0)


def joined_along(parts, dim):
    shape = list(parts.shape[1:])
    shape[dim] *= parts.shape[0]
    return jnp.moveaxis(parts, 0, dim).reshape(shape)


def one_exchange(array, axis, axes, splits, concats):
    sizes = [lax.axis_size(a) for a in axes]
    parts = split_up(array, splits[0], sizes[0])
    parts = jnp.moveaxis(split_up(parts, splits[1] + 1, sizes[1]), 0, 1)
    inside = parts.shape[2:]
    parts = parts.reshape(-1, *inside)
    parts = lax.all_to_all(parts, axis, split_axis=0, concat_axis=0, tiled=True)
    parts = joined_along(parts.reshape(*sizes, *inside), concats[0] + 1)
    return joined_along(parts, concats[1])


def slot_rank(block_ids):
    count = block_ids.shape[0]
    same = block_ids[:, None] == block_ids[None, :]
    earlier = (
        jnp.arange(count, dtype=jnp.int32)[None, :] < jnp.arange(count, dtype=jnp.int32)[:, None]
    )
    return jnp.sum((same & earlier).astype(jnp.int32), axis=1)


def run_expert(received, first, second):
    lead = received.shape[:-1]
    width = received.shape[-1]
    flat_rows = received.reshape(-1, width)
    hidden = jnp.maximum(jnp.dot(flat_rows, first, preferred_element_type=jnp.float32), 0.0).astype(
        jnp.bfloat16
    )
    answer = jnp.dot(hidden, second, preferred_element_type=jnp.float32).astype(jnp.bfloat16)
    return answer.reshape(lead + (width,))


def on_device(tokens, expert_ids, gate_prob, norm_gain, weight_in, weight_out):
    tok_rows, width = tokens.shape
    row_count = lax.axis_size(ROW)
    col_count = lax.axis_size(COL)
    experts = row_count * col_count
    capacity = 2 * tok_rows // experts
    local_ids = expert_ids[:, 0]
    within = slot_rank(local_ids)
    placed = local_ids * capacity + within
    wide = tokens.astype(jnp.float32)
    scale = lax.rsqrt(jnp.mean(wide * wide, axis=1, keepdims=True) + 1e-06)
    normed = (wide * scale * norm_gain[None, :]).astype(jnp.bfloat16)
    matches = (local_ids[:, None] == jnp.arange(experts, dtype=jnp.int32)[None, :]).astype(
        jnp.float32
    )
    counts = jnp.sum(matches, axis=0)
    routed = sum_in_two_steps(counts, (("row_0", "row_1", "col_0"), "col_1"), 0).astype(jnp.int32)
    table = (placed[None, :] == jnp.arange(experts * capacity, dtype=jnp.int32)[:, None]).astype(
        jnp.bfloat16
    )
    outgoing = jnp.dot(table, normed, preferred_element_type=jnp.float32).astype(jnp.bfloat16)
    first = weight_in[0]
    second = weight_out[0]
    grid_out = outgoing.reshape(row_count, col_count, capacity, width)
    arrived = one_exchange(grid_out, ROW_COL, (ROW, COL), (0, 1), (0, 1))
    answers = run_expert(arrived, first, second)
    returned = one_exchange(answers, ROW_COL, (ROW, COL), (0, 1), (0, 1))
    returned = returned.reshape(experts * capacity, width)
    back = jnp.einsum("st,sd->td", table, returned, preferred_element_type=jnp.float32)
    mixed = (wide + gate_prob[:, None] * back).astype(jnp.bfloat16)
    return (mixed, routed)


def solution(mesh):
    finer = Mesh(mesh.devices.reshape(4, 2, 4, 4), ("row_0", "row_1", "col_0", "col_1"))
    return jax.shard_map(
        on_device,
        mesh=finer,
        in_specs=(
            P(ROW_COL, None),
            P(ROW_COL, None),
            P(ROW_COL),
            P(),
            P(ROW_COL, None, None),
            P(ROW_COL, None, None),
        ),
        out_specs=(P(ROW_COL, None), P(ROW_COL)),
        check_vma=False,
    )
```

profile of v0, /device:TPU:0, one launch (start us, length us, event | category | flops | bytes accessed | tf_op | source)
XLA Modules:
  0.0 125.0 jit_solution(17238979280621386907)
XLA Ops:
  0.6 0.8 convert_reduce_fusion.1
  1.5 0.1 reshape_reshape.11
  1.6 0.7 copy.14
  2.2 5.4 %all-to-all-start.2 = ((f32[4,32,1]{1,2,0:T(1,128)}), f32[4,32,1]{1,2,0:T(1,128)S(1)}, u32[]{:S(2)}, u32[]{:S(2)}) async-start(f32[4,32,1]{1,2,0:T(1,128)} %copy.14), calls=%async_computation.2 | async-start | bytes 4096 | tf_op jit(solution)/shard_map/all_to_all | solution.py:19
  7.6 1.0 convert_reduce_fusion
  8.6 0.7 multiply_add_fusion
  9.3 1.5 %fusion.5 = f32[512]{0:T(512)S(1)} fusion(bf16[512,1024]{1,0:T(8,128)(2,1)} %param.6), kind=kLoop, calls=%fused_computation.7 | loop fusion | flops 1572352 | bytes 1050624 | tf_op jit(solution)/shard_map/reduce_sum | solution.py:76
  10.8 4.0 %convert_bitcast_fusion.1 = bf16[128,1,1,8,1024]{4,3,2,1,0:T(8,128)(2,1)} fusion(bf16[512,1024]{1,0:T(8,128)(2,1)} %param.6, f32[1024]{0:T(1024)} %param.9, f32[512]{0:T(512)S(1)} %add_rsqrt_fusion, s32[512]{0:T(512)S(1)} %multiply_add_fusion), kind=kOutput, calls=%fused_computation.15 | convolution fusion | flops 1077411840 | bytes 3153920 | tf_op jit(solution)/shard_map/dot_general | solution.py:86
  14.8 0.0 all-to-all-done.2
  14.8 10.6 %all-to-all-start = ((bf16[128,1,1,8,1024]{4,3,2,1,0:T(8,128)(2,1)}), bf16[128,1,1,8,1024]{4,3,2,1,0:T(8,128)(2,1)S(1)}, u32[]{:S(2)}, u32[]{:S(2)}) async-start(bf16[128,1,1,8,1024]{4,3,2,1,0:T(8,128)(2,1)} %convert_bitcast_fusion.1), calls=%async_computation | async-start | bytes 4194304 | tf_op jit(solution)/shard_map/all_to_all | solution.py:41
  25.4 0.7 copy.15
  26.1 29.1 %all-to-all-done = bf16[128,1,1,8,1024]{4,3,2,1,0:T(8,128)(2,1)S(1)} async-done(((bf16[128,1,1,8,1024]{4,3,2,1,0:T(8,128)(2,1)}), bf16[128,1,1,8,1024]{4,3,2,1,0:T(8,128)(2,1)S(1)}, u32[]{:S(2)}, u32[]{:S(2)}) %all-to-all-start) | async-done | bytes 2097184 | tf_op jit(solution)/shard_map/all_to_all | solution.py:41
  55.2 4.1 %all-to-all-start.3 = ((f32[32,1,1]{2,1,0:T(1,128)}), f32[32,1,1]{2,1,0:T(1,128)S(1)}, u32[]{:S(2)}, u32[]{:S(2)}) async-start(f32[32,1,1]{2,1,0:T(1,128)} %copy.15), calls=%async_computation.3 | async-start | bytes 32768 | tf_op jit(solution)/shard_map/all_to_all | solution.py:26
  59.3 24.6 %convert_bitcast_fusion = bf16[128,1,1,8,1024]{4,3,2,1,0:T(8,128)(2,1)} fusion(bf16[1,4096,1024]{2,1,0:T(8,128)(2,1)} %param.11, bf16[1,1024,4096]{2,1,0:T(8,128)(2,1)} %param.10, bf16[128,1,1,8,1024]{4,3,2,1,0:T(8,128)(2,1)S(1)} %all-to-all-done), kind=kOutput, calls=%fused_computation.14 | convolution fusion | flops 17189306368 | bytes 20971520 | tf_op jit(solution)/shard_map/dot_general | solution.py:62
  83.9 0.0 copy-start
  83.9 0.0 copy-start.1
  83.9 0.0 all-to-all-done.3
  83.9 8.0 %all-to-all-start.1 = ((bf16[128,1,1,8,1024]{4,3,2,1,0:T(8,128)(2,1)}), bf16[128,1,1,8,1024]{4,3,2,1,0:T(8,128)(2,1)S(1)}, u32[]{:S(2)}, u32[]{:S(2)}) async-start(bf16[128,1,1,8,1024]{4,3,2,1,0:T(8,128)(2,1)} %convert_bitcast_fusion), calls=%async_computation.1 | async-start | bytes 4194304 | tf_op jit(solution)/shard_map/all_to_all | solution.py:41
  91.9 0.6 reduce_sum.49
  93.1 28.5 %all-to-all-done.1 = bf16[128,1,1,8,1024]{4,3,2,1,0:T(8,128)(2,1)S(1)} async-done(((bf16[128,1,1,8,1024]{4,3,2,1,0:T(8,128)(2,1)}), bf16[128,1,1,8,1024]{4,3,2,1,0:T(8,128)(2,1)S(1)}, u32[]{:S(2)}, u32[]{:S(2)}) %all-to-all-start.1) | async-done | bytes 2097184 | tf_op jit(solution)/shard_map/all_to_all | solution.py:41
  121.6 0.0 copy-done
  121.6 0.0 copy-done.1
  121.6 2.3 %fusion.8 = bf16[512,1024]{1,0:T(8,128)(2,1)} fusion(bf16[512,1024]{1,0:T(8,128)(2,1)S(1)} %copy-done, bf16[128,1,1,8,1024]{4,3,2,1,0:T(8,128)(2,1)S(1)} %all-to-all-done.1, s32[512]{0:T(512)S(1)} %multiply_add_fusion, f32[512]{0:T(512)S(1)} %copy-done.1), kind=kOutput, calls=%fused_computation.10 | convolution fusion | flops 1076363264 | bytes 4198400 | tf_op jit(solution)/shard_map/st,sd->td/dot_general | solution.py:94
  (2 shorter events, 0.0 us)
Async XLA Ops:
  2.2 12.6 %all-to-all-start.2 = ((f32[4,32,1]{1,2,0:T(1,128)}), f32[4,32,1]{1,2,0:T(1,128)S(1)}, u32[]{:S(2)}, u32[]{:S(2)}) async-start(f32[4,32,1]{1,2,0:T(1,128)} %copy.14), calls=%async_computation.2 | async-start | bytes 4096 | tf_op jit(solution)/shard_map/all_to_all | solution.py:19
  14.8 40.3 %all-to-all-start = ((bf16[128,1,1,8,1024]{4,3,2,1,0:T(8,128)(2,1)}), bf16[128,1,1,8,1024]{4,3,2,1,0:T(8,128)(2,1)S(1)}, u32[]{:S(2)}, u32[]{:S(2)}) async-start(bf16[128,1,1,8,1024]{4,3,2,1,0:T(8,128)(2,1)} %convert_bitcast_fusion.1), calls=%async_computation | async-start | bytes 4194304 | tf_op jit(solution)/shard_map/all_to_all | solution.py:41
  55.2 28.7 %all-to-all-start.3 = ((f32[32,1,1]{2,1,0:T(1,128)}), f32[32,1,1]{2,1,0:T(1,128)S(1)}, u32[]{:S(2)}, u32[]{:S(2)}) async-start(f32[32,1,1]{2,1,0:T(1,128)} %copy.15), calls=%async_computation.3 | async-start | bytes 32768 | tf_op jit(solution)/shard_map/all_to_all | solution.py:26
  83.9 37.8 %copy-start = (bf16[512,1024]{1,0:T(8,128)(2,1)S(1)}, bf16[512,1024]{1,0:T(8,128)(2,1)}, u32[]{:S(2)}) copy-start(bf16[512,1024]{1,0:T(8,128)(2,1)} %param.6) | copy-start | bytes 3145732
  83.9 37.8 %copy-start.1 = (f32[512]{0:T(512)S(1)}, f32[512]{0:T(512)}, u32[]{:S(2)}) copy-start(f32[512]{0:T(512)} %param.8) | copy-start | bytes 6148
  83.9 37.8 %all-to-all-start.1 = ((bf16[128,1,1,8,1024]{4,3,2,1,0:T(8,128)(2,1)}), bf16[128,1,1,8,1024]{4,3,2,1,0:T(8,128)(2,1)S(1)}, u32[]{:S(2)}, u32[]{:S(2)}) async-start(bf16[128,1,1,8,1024]{4,3,2,1,0:T(8,128)(2,1)} %convert_bitcast_fusion), calls=%async_computation.1 | async-start | bytes 4194304 | tf_op jit(solution)/shard_map/all_to_all | solution.py:41
where the time goes:
time: 126 us; the launch traced here: 125 us
  waiting for transfers between devices  57.5 us (46%)
  matrix products  30.8 us (24%)
  starting transfers between devices  28.1 us (22%)
  other arithmetic  4.69 us (4%)
  between operations  2.46 us (2%)
  local copies, waits for them, and re-layouts  1.46 us (1%)
    all_to_all x2, waiting for transfers between devices, one_exchange(): parts = lax.all_to_all(parts, axis, split_axis=0, concat_axis=0, tiled=True)  57.5 us
    dot_general x1, matrix products, run_expert(): jnp.dot(hidden, second, preferred_element_type=jnp.float32)  24.6 us
    all_to_all x2, starting transfers between devices, one_exchange(): parts = lax.all_to_all(parts, axis, split_axis=0, concat_axis=0, tiled=True)  18.5 us
    all_to_all x1, starting transfers between devices, sent_and_summed(): lax.all_to_all(parts, axis, split_axis=0, concat_axis=0, tiled=True)  5.42 us
    all_to_all x1, starting transfers between devices, sum_in_two_steps(): return jnp.sum(lax.all_to_all(own, far, 0, 0, tiled=True), axis=0)  4.11 us
    dot_general x1, matrix products, on_device(): jnp.dot(table, normed, preferred_element_type=jnp.float32)  3.98 us
  transfers between devices with their start and end apart: 4, of which 2 were waited for; matrix products, arithmetic and copies ran while one was open for 26% of the time, Pallas kernels for 0%

commit v1 on v0

--- a/solution.py
+++ b/solution.py
@@ -7,23 +7,12 @@
 ROW = ("row_0", "row_1")
 COL = ("col_0", "col_1")
 ROW_COL = ("row_0", "row_1", "col_0", "col_1")
+EMPTY = 32768.0
 
 
 def split_up(array, dim, peers):
     before, after = (array.shape[:dim], array.shape[dim + 1 :])
     return jnp.moveaxis(array.reshape(*before, peers, -1, *after), dim, 0)
-
-
-def sent_and_summed(array, axis, dim):
-    parts = split_up(array, dim, lax.axis_size(axis))
-    arrived = lax.all_to_all(parts, axis, split_axis=0, concat_axis=0, tiled=True)
-    return arrived.sum(axis=0)
-
-
-def sum_in_two_steps(array, axes, dim):
-    far, near = axes
-    own = sent_and_summed(split_up(array, dim, lax.axis_size(far)), near, dim + 1)
-    return jnp.sum(lax.all_to_all(own, far, 0, 0, tiled=True), axis=0)
 
 
 def joined_along(parts, dim):
@@ -75,19 +64,23 @@
     wide = tokens.astype(jnp.float32)
     scale = lax.rsqrt(jnp.mean(wide * wide, axis=1, keepdims=True) + 1e-06)
     normed = (wide * scale * norm_gain[None, :]).astype(jnp.bfloat16)
-    matches = (local_ids[:, None] == jnp.arange(experts, dtype=jnp.int32)[None, :]).astype(
-        jnp.float32
-    )
-    counts = jnp.sum(matches, axis=0)
-    routed = sum_in_two_steps(counts, (("row_0", "row_1", "col_0"), "col_1"), 0).astype(jnp.int32)
     table = (placed[None, :] == jnp.arange(experts * capacity, dtype=jnp.int32)[:, None]).astype(
         jnp.bfloat16
     )
     outgoing = jnp.dot(table, normed, preferred_element_type=jnp.float32).astype(jnp.bfloat16)
+    taken = jnp.sum(
+        (local_ids[:, None] == jnp.arange(experts, dtype=jnp.int32)[None, :]).astype(jnp.int32),
+        axis=0,
+    )
+    empty = jnp.arange(capacity, dtype=jnp.int32)[None, :] >= taken[:, None]
+    empty = empty.reshape(-1)[:, None] & (jnp.arange(width, dtype=jnp.int32)[None, :] < 128)
+    outgoing = jnp.where(empty, jnp.bfloat16(EMPTY), outgoing)
     first = weight_in[0]
     second = weight_out[0]
     grid_out = outgoing.reshape(row_count, col_count, capacity, width)
     arrived = one_exchange(grid_out, ROW_COL, (ROW, COL), (0, 1), (0, 1))
+    marks = arrived[..., 0].astype(jnp.float32)
+    routed = jnp.sum((marks < 0.5 * EMPTY).astype(jnp.int32)).reshape(1)
     answers = run_expert(arrived, first, second)
     returned = one_exchange(answers, ROW_COL, (ROW, COL), (0, 1), (0, 1))
     returned = returned.reshape(experts * capacity, width)

time: 126 us -> 143 us (1.13)
  blocking collectives: 0 us -> 40.8 us
  local copies, waits for them, and re-layouts: 1.46 us -> 32.5 us
  waiting for transfers between devices: 57.5 us -> 28.4 us
  starting transfers between devices: 28.1 us -> 4.78 us
  between operations: 2.46 us -> 0.67 us
    all_to_all x0 -> x1, blocking collectives: none -> 40.8 us  [one_exchange(): parts = lax.all_to_all(parts, axis, split_axis=0, concat_axis=0, tiled=True)]
    all_to_all x2 -> x1, waiting for transfers between devices: 57.5 us -> 28.4 us  [one_exchange(): parts = lax.all_to_all(parts, axis, split_axis=0, concat_axis=0, tiled=True)]
    transpose x1, local copies, waits for them, and re-layouts: 0.66 us -> 17.7 us  [joined_along(): return jnp.moveaxis(parts, 0, dim).reshape(shape)]
    reshape x0 -> x1, local copies, waits for them, and re-layouts: none -> 14.7 us  [one_exchange(): parts = joined_along(parts.reshape(*sizes, *inside), concats[0] + 1)]
    all_to_all x2 -> x1, starting transfers between devices: 18.5 us -> 4.78 us  [one_exchange(): parts = lax.all_to_all(parts, axis, split_axis=0, concat_axis=0, tiled=True)]
    all_to_all x2 -> x0, starting transfers between devices: 9.53 us -> none  [the longest x1 5.42 us: sent_and_summed(): lax.all_to_all(parts, axis, split_axis=0, concat_axis=0, tiled=True)]
  transfers between devices with their start and end apart: 4 -> 1, of which waited for: 2 -> 1; matrix products, arithmetic and copies ran while one was open for 26% -> 1% of each run, Pallas kernels for 0% -> 0%
where the time goes in v1:
time: 143 us; the launch traced here: 142 us
  blocking collectives  40.8 us (29%)
  local copies, waits for them, and re-layouts  32.5 us (23%)
  matrix products  29.6 us (21%)
  waiting for transfers between devices  28.4 us (20%)
  other arithmetic  5.5 us (4%)
  starting transfers between devices  4.78 us (3%)
    all_to_all x1, blocking collectives, one_exchange(): parts = lax.all_to_all(parts, axis, split_axis=0, concat_axis=0, tiled=True)  40.8 us
    all_to_all x1, waiting for transfers between devices, one_exchange(): parts = lax.all_to_all(parts, axis, split_axis=0, concat_axis=0, tiled=True)  28.4 us
    dot_general x1, matrix products, run_expert(): jnp.dot(hidden, second, preferred_element_type=jnp.float32)  24.6 us
    transpose x1, local copies, waits for them, and re-layouts, joined_along(): return jnp.moveaxis(parts, 0, dim).reshape(shape)  17.7 us
    reshape x1, local copies, waits for them, and re-layouts, one_exchange(): parts = joined_along(parts.reshape(*sizes, *inside), concats[0] + 1)  14.7 us
    all_to_all x1, starting transfers between devices, one_exchange(): parts = lax.all_to_all(parts, axis, split_axis=0, concat_axis=0, tiled=True)  4.78 us
  transfers between devices with their start and end apart: 1, of which 1 were waited for; matrix products, arithmetic and copies ran while one was open for 1% of the time, Pallas kernels for 0%

profile of v1, /device:TPU:0, one launch (start us, length us, event | category | flops | bytes accessed | tf_op | source)
XLA Modules:
  0.0 142.2 jit_solution(15745230252953168632)
XLA Ops:
  0.6 0.8 convert_reduce_fusion.1
  1.5 1.0 convert_reduce_fusion
  2.5 0.7 multiply_add_fusion
  3.2 1.5 %fusion.5 = f32[512]{0:T(512)S(1)} fusion(bf16[512,1024]{1,0:T(8,128)(2,1)} %param.6), kind=kLoop, calls=%fused_computation.8 | loop fusion | flops 1572352 | bytes 1050624 | tf_op jit(solution)/shard_map/reduce_sum | solution.py:65
  4.7 0.1 iota_compare_fusion.9
  4.8 0.1 ge.23
  4.9 2.7 %fusion.9 = bf16[128,1,1,8,1024]{4,3,2,1,0:T(8,128)(2,1)S(1)} fusion(pred[1024]{0:T(1024)(128)(4,1)S(1)} %iota_compare_fusion.10, pred[1024]{0:T(1024)(128)(4,1)S(1)} %ge.23, bf16[512,1024]{1,0:T(8,128)(2,1)} %param.6, f32[1024]{0:T(1024)} %param.9, f32[512]{0:T(512)S(1)} %add_rsqrt_fusion, s32[512]{0:T(512)S(1)} %multiply_add_fusion), kind=kOutput, calls=%fused_computation.12 | convolution fusion | flops 1079508992 | bytes 3155968 | tf_op jit(solution)/shard_map/dot_general | solution.py:70
  7.6 40.8 %all_to_all.10 = bf16[128,1,1,8,1024]{4,3,2,1,0:T(8,128)(2,1)S(1)} all-to-all(bf16[128,1,1,8,1024]{4,3,2,1,0:T(8,128)(2,1)S(1)} %fusion.9), channel_id=1, replica_groups=mesh['row_0'=4,'row_1'=2,'col_0'=4,'col_1'=4] {'row_0','row_1','col_0','..., dimensions={0} | all-to-all | bytes 4194304 | tf_op jit(solution)/shard_map/all_to_all | solution.py:30
  48.4 14.7 %copy.15 = bf16[8,16,1,1,8,1024]{1,4,5,0,3,2:T(8,128)(2,1)} copy(bf16[8,16,1,1,8,1024]{5,4,1,0,3,2:T(8,128)(2,1)S(1)} %bitcast.47) | data formatting | bytes 4194304 | tf_op jit(solution)/shard_map/reshape | solution.py:31
  63.0 17.7 %copy.16 = bf16[8,16,1,8,1024]{4,3,1,0,2:T(8,128)(2,1)S(1)} copy(bf16[8,16,1,8,1024]{1,3,4,0,2:T(8,128)(2,1)} %bitcast.45) | data formatting | bytes 4194304 | tf_op jit(solution)/shard_map/transpose | solution.py:21
  80.7 24.6 %convert_bitcast_fusion = bf16[128,1,1,8,1024]{4,3,2,1,0:T(8,128)(2,1)} fusion(bf16[1,4096,1024]{2,1,0:T(8,128)(2,1)} %param.11, bf16[1024,1024]{1,0:T(8,128)(2,1)S(1)} %bitcast.48, bf16[1,1024,4096]{2,1,0:T(8,128)(2,1)} %param.10), kind=kOutput, calls=%fused_computation.15 | convolution fusion | flops 17189306368 | bytes 20971520 | tf_op jit(solution)/shard_map/dot_general | solution.py:51
  105.3 0.0 copy-start
  105.3 0.0 copy-start.1
  105.3 4.8 %all-to-all-start.1 = ((bf16[128,1,1,8,1024]{4,3,2,1,0:T(8,128)(2,1)}), bf16[128,1,1,8,1024]{4,3,2,1,0:T(8,128)(2,1)S(1)}, u32[]{:S(2)}, u32[]{:S(2)}) async-start(bf16[128,1,1,8,1024]{4,3,2,1,0:T(8,128)(2,1)} %convert_bitcast_fusion), calls=%async_computation.1 | async-start | bytes 4194304 | tf_op jit(solution)/shard_map/all_to_all | solution.py:30
  110.1 1.4 convert_reduce_fusion.2
  111.5 28.4 %all-to-all-done.1 = bf16[128,1,1,8,1024]{4,3,2,1,0:T(8,128)(2,1)S(1)} async-done(((bf16[128,1,1,8,1024]{4,3,2,1,0:T(8,128)(2,1)}), bf16[128,1,1,8,1024]{4,3,2,1,0:T(8,128)(2,1)S(1)}, u32[]{:S(2)}, u32[]{:S(2)}) %all-to-all-start.1) | async-done | bytes 2097184 | tf_op jit(solution)/shard_map/all_to_all | solution.py:30
  139.9 0.0 copy-done
  139.9 0.0 copy-done.1
  139.9 2.3 %fusion.8 = bf16[512,1024]{1,0:T(8,128)(2,1)} fusion(bf16[512,1024]{1,0:T(8,128)(2,1)S(1)} %copy-done, bf16[128,1,1,8,1024]{4,3,2,1,0:T(8,128)(2,1)S(1)} %all-to-all-done.1, s32[512]{0:T(512)S(1)} %multiply_add_fusion, f32[512]{0:T(512)S(1)} %copy-done.1), kind=kOutput, calls=%fused_computation.11 | convolution fusion | flops 1076363264 | bytes 4198400 | tf_op jit(solution)/shard_map/st,sd->td/dot_general | solution.py:87
  (2 shorter events, 0.0 us)
Async XLA Ops:
  105.3 34.6 %copy-start = (bf16[512,1024]{1,0:T(8,128)(2,1)S(1)}, bf16[512,1024]{1,0:T(8,128)(2,1)}, u32[]{:S(2)}) copy-start(bf16[512,1024]{1,0:T(8,128)(2,1)} %param.6) | copy-start | bytes 3145732
  105.3 34.6 %copy-start.1 = (f32[512]{0:T(512)S(1)}, f32[512]{0:T(512)}, u32[]{:S(2)}) copy-start(f32[512]{0:T(512)} %param.8) | copy-start | bytes 6148
  105.3 34.6 %all-to-all-start.1 = ((bf16[128,1,1,8,1024]{4,3,2,1,0:T(8,128)(2,1)}), bf16[128,1,1,8,1024]{4,3,2,1,0:T(8,128)(2,1)S(1)}, u32[]{:S(2)}, u32[]{:S(2)}) async-start(bf16[128,1,1,8,1024]{4,3,2,1,0:T(8,128)(2,1)} %convert_bitcast_fusion), calls=%async_computation.1 | async-start | bytes 4194304 | tf_op jit(solution)/shard_map/all_to_all | solution.py:30

commit v2 on v1

v2 whole, which is shorter than its diff:
```python
import jax
import jax.numpy as jnp
from jax import lax
from jax.experimental import pallas as pl
from jax.experimental.pallas import tpu as pltpu
from jax.sharding import Mesh
from jax.sharding import PartitionSpec as P

ROW_COL = ("row_0", "row_1", "col_0", "col_1")
EMPTY = 32768.0
MARKED = 128
DISPATCH_COLS = 256
FF_BLOCK = 512
COMBINE_COLS = 256


def one_hot(match):
    return jnp.where(match, 1.0, 0.0).astype(jnp.bfloat16)


def dispatch_kernel(tok_ref, ids_ref, gain_ref, out_ref, placed_ref, table_ref, normed_ref):
    slots, count = table_ref.shape
    cols = out_ref.shape[1]
    step = pl.program_id(0)

    @pl.when(step == 0)
    def _():
        ids = ids_ref[...]
        experts = 128
        capacity = slots // experts
        match = lax.broadcasted_iota(jnp.int32, (experts, count), 0) == ids
        before = lax.broadcasted_iota(jnp.int32, (count, count), 0) < lax.broadcasted_iota(
            jnp.int32, (count, count), 1
        )
        earlier = jnp.dot(one_hot(match), one_hot(before), preferred_element_type=jnp.float32)
        within = jnp.sum(jnp.where(match, earlier, 0.0), axis=0, keepdims=True)
        placed = ids * capacity + within.astype(jnp.int32)
        placed_ref[...] = placed
        table_ref[...] = one_hot(lax.broadcasted_iota(jnp.int32, (slots, count), 0) == placed)
        wide = tok_ref[...].astype(jnp.float32)
        scale = lax.rsqrt(jnp.mean(wide * wide, axis=1, keepdims=True) + 1e-06)
        normed_ref[...] = (wide * scale * gain_ref[...]).astype(jnp.bfloat16)

    table = table_ref[...]
    start = pl.multiple_of(step * cols, cols)
    sent = jnp.dot(table, normed_ref[:, pl.ds(start, cols)], preferred_element_type=jnp.float32)
    out_ref[...] = sent.astype(jnp.bfloat16)

    @pl.when(step == 0)
    def _():
        filled = jnp.dot(
            table, jnp.ones((count, MARKED), jnp.bfloat16), preferred_element_type=jnp.float32
        )
        out_ref[:, :MARKED] = jnp.where(filled > 0.5, sent[:, :MARKED], EMPTY).astype(jnp.bfloat16)


def dispatch(tokens, ids, gain, slots):
    count, width = tokens.shape
    cols = DISPATCH_COLS
    return pl.pallas_call(
        dispatch_kernel,
        grid=(width // cols,),
        in_specs=[
            pl.BlockSpec((count, width), lambda j: (0, 0)),
            pl.BlockSpec((1, count), lambda j: (0, 0)),
            pl.BlockSpec((1, width), lambda j: (0, 0)),
        ],
        out_specs=[
            pl.BlockSpec((slots, cols), lambda j: (0, j)),
            pl.BlockSpec((1, count), lambda j: (0, 0)),
        ],
        out_shape=[
            jax.ShapeDtypeStruct((slots, width), jnp.bfloat16),
            jax.ShapeDtypeStruct((1, count), jnp.int32),
        ],
        scratch_shapes=[
            pltpu.VMEM((slots, count), jnp.bfloat16),
            pltpu.VMEM((count, width), jnp.bfloat16),
        ],
        cost_estimate=pl.CostEstimate(
            flops=2 * slots * count * width, bytes_accessed=4 * slots * width, transcendentals=0
        ),
        name="dispatch",
    )(tokens, ids, gain)


def prepare_kernel(placed_ref, gate_ref, table_ref, gates_ref):
    count, slots = table_ref.shape
    lanes = gates_ref.shape[1]
    rows = jnp.broadcast_to(placed_ref[...].astype(jnp.float32), (lanes, count)).T.astype(jnp.int32)
    gates_ref[...] = jnp.broadcast_to(gate_ref[...], (lanes, count)).T
    lane = lax.broadcasted_iota(jnp.int32, (count, lanes), 1)
    for start in range(0, slots, lanes):
        table_ref[:, start : start + lanes] = one_hot(lane + start == rows)


def prepare(placed, gate, slots):
    count = placed.shape[1]
    return pl.pallas_call(
        prepare_kernel,
        out_shape=[
            jax.ShapeDtypeStruct((count, slots), jnp.bfloat16),
            jax.ShapeDtypeStruct((count, 128), jnp.float32),
        ],
        cost_estimate=pl.CostEstimate(
            flops=4 * slots * count, bytes_accessed=2 * slots * count, transcendentals=0
        ),
        name="prepare",
    )(placed, gate)


def expert_kernel(x_ref, first_ref, second_ref, out_ref, routed_ref, total_ref):
    step = pl.program_id(0)

    @pl.when(step == 0)
    def _():
        kept = jnp.where(x_ref[:, :MARKED].astype(jnp.float32) < 0.5 * EMPTY, 1.0, 0.0)
        routed_ref[0] = jnp.sum(kept).astype(jnp.int32) // MARKED

    hidden = jnp.maximum(
        jnp.dot(x_ref[...], first_ref[...], preferred_element_type=jnp.float32), 0.0
    ).astype(jnp.bfloat16)
    part = jnp.dot(hidden, second_ref[...], preferred_element_type=jnp.float32)

    @pl.when(step == 0)
    def _():
        total_ref[...] = part

    @pl.when((step > 0) & (step < pl.num_programs(0) - 1))
    def _():
        total_ref[...] += part

    @pl.when(step == pl.num_programs(0) - 1)
    def _():
        out_ref[...] = (total_ref[...] + part).astype(jnp.bfloat16)


def expert(x, first, second):
    rows, width = x.shape
    ff = first.shape[1]
    return pl.pallas_call(
        expert_kernel,
        grid=(ff // FF_BLOCK,),
        in_specs=[
            pl.BlockSpec((rows, width), lambda j: (0, 0)),
            pl.BlockSpec((width, FF_BLOCK), lambda j: (0, j)),
            pl.BlockSpec((FF_BLOCK, width), lambda j: (j, 0)),
        ],
        out_specs=[
            pl.BlockSpec((rows, width), lambda j: (0, 0)),
            pl.BlockSpec(memory_space=pltpu.SMEM),
        ],
        out_shape=[
            jax.ShapeDtypeStruct((rows, width), jnp.bfloat16),
            jax.ShapeDtypeStruct((1,), jnp.int32),
        ],
        scratch_shapes=[pltpu.VMEM((rows, width), jnp.float32)],
        cost_estimate=pl.CostEstimate(
            flops=4 * rows * width * ff, bytes_accessed=4 * width * (ff + rows), transcendentals=0
        ),
        name="expert",
    )(x, first, second)


def combine_kernel(table_ref, back_ref, gates_ref, tok_ref, out_ref):
    back = jnp.dot(table_ref[...], back_ref[...], preferred_element_type=jnp.float32)
    gates = jnp.concatenate([gates_ref[...]] * (back.shape[1] // gates_ref.shape[1]), axis=1)
    out_ref[...] = (tok_ref[...].astype(jnp.float32) + gates * back).astype(jnp.bfloat16)


def combine(table, back, gates, tokens):
    count, width = tokens.shape
    slots = back.shape[0]
    cols = COMBINE_COLS
    return pl.pallas_call(
        combine_kernel,
        grid=(width // cols,),
        in_specs=[
            pl.BlockSpec((count, slots), lambda j: (0, 0)),
            pl.BlockSpec((slots, cols), lambda j: (0, j)),
            pl.BlockSpec(gates.shape, lambda j: (0, 0)),
            pl.BlockSpec((count, cols), lambda j: (0, j)),
        ],
        out_specs=pl.BlockSpec((count, cols), lambda j: (0, j)),
        out_shape=jax.ShapeDtypeStruct((count, width), jnp.bfloat16),
        cost_estimate=pl.CostEstimate(
            flops=2 * slots * count * width, bytes_accessed=4 * slots * width, transcendentals=0
        ),
        name="combine",
    )(table, back, gates, tokens)


def exchange(rows, devices):
    parts = rows.reshape(devices, rows.shape[0] // devices, rows.shape[1])
    parts = lax.all_to_all(parts, ROW_COL, split_axis=0, concat_axis=0, tiled=True)
    return parts.reshape(rows.shape)


def on_device(tokens, expert_ids, gate_prob, norm_gain, weight_in, weight_out):
    tok_rows, width = tokens.shape
    experts = lax.axis_size(ROW_COL)
    slots = 2 * tok_rows
    ids = expert_ids.reshape(1, tok_rows)
    outgoing, placed = dispatch(tokens, ids, norm_gain.reshape(1, width), slots)
    arrived = exchange(outgoing, experts)
    table, gates = prepare(placed, gate_prob.reshape(1, tok_rows), slots)
    answers, routed = expert(arrived, weight_in[0], weight_out[0])
    returned = exchange(answers, experts)
    mixed = combine(table, returned, gates, tokens)
    return (mixed, routed)


def solution(mesh):
    finer = Mesh(mesh.devices.reshape(4, 2, 4, 4), ROW_COL)
    return jax.shard_map(
        on_device,
        mesh=finer,
        in_specs=(
            P(ROW_COL, None),
            P(ROW_COL, None),
            P(ROW_COL),
            P(),
            P(ROW_COL, None, None),
            P(ROW_COL, None, None),
        ),
        out_specs=(P(ROW_COL, None), P(ROW_COL)),
        check_vma=False,
    )
```

time: 143 us -> 115 us (0.80)
  Pallas kernels: 0 us -> 38.9 us
  local copies, waits for them, and re-layouts: 32.5 us -> 1.34 us
  matrix products: 29.6 us -> 0 us
  other arithmetic: 5.5 us -> 0 us
    pallas_call x0 -> x4, Pallas kernels: none -> 38.9 us  [the longest x1 26.2 us: expert(): pl.pallas_call(expert_kernel, grid=(ff // FF_BLOCK,), in_specs=[pl.BlockS...]
    dot_general x3 -> x0, matrix products: 29.6 us -> none  [the longest x1 24.6 us: run_expert(): jnp.dot(hidden, second, preferred_element_type=jnp.float32)]
    transpose x1 -> x0, local copies, waits for them, and re-layouts: 17.7 us -> none  [joined_along(): return jnp.moveaxis(parts, 0, dim).reshape(shape)]
    reshape x1 -> x0, local copies, waits for them, and re-layouts: 14.7 us -> none  [one_exchange(): parts = joined_along(parts.reshape(*sizes, *inside), concats[0] + 1)]
    reduce_sum x4 -> x0, other arithmetic: 4.7 us -> none  [the longest x1 1.5 us: on_device(): scale = lax.rsqrt(jnp.mean(wide * wide, axis=1, keepdims=True) + 1e-06)]
  transfers between devices with their start and end apart: 1 -> 1, of which waited for: 1 -> 1; matrix products, arithmetic and copies ran while one was open for 1% -> 0% of each run, Pallas kernels for 0% -> 2%
where the time goes in v2:
time: 115 us; the launch traced here: 114 us
  blocking collectives  41.1 us (36%)
  Pallas kernels  38.9 us (34%)
  waiting for transfers between devices  27.7 us (24%)
  starting transfers between devices  4.67 us (4%)
  local copies, waits for them, and re-layouts  1.34 us (1%)
    all_to_all x1, blocking collectives, exchange(): lax.all_to_all(parts, ROW_COL, split_axis=0, concat_axis=0, tiled=True)  41.1 us
    all_to_all x1, waiting for transfers between devices, exchange(): lax.all_to_all(parts, ROW_COL, split_axis=0, concat_axis=0, tiled=True)  27.7 us
    pallas_call x1, Pallas kernels, expert(): pl.pallas_call(expert_kernel, grid=(ff // FF_BLOCK,), in_specs=[pl.BlockS...  26.2 us
    pallas_call x1, Pallas kernels, dispatch(): pl.pallas_call(dispatch_kernel, grid=(width // cols,), in_specs=[pl.Block...  5.7 us
    pallas_call x1, Pallas kernels, combine(): pl.pallas_call(combine_kernel, grid=(width // cols,), in_specs=[pl.BlockS...  5.02 us
    all_to_all x1, starting transfers between devices, exchange(): lax.all_to_all(parts, ROW_COL, split_axis=0, concat_axis=0, tiled=True)  4.67 us
  transfers between devices with their start and end apart: 1, of which 1 were waited for; matrix products, arithmetic and copies ran while one was open for 0% of the time, Pallas kernels for 2%

profile of v2, /device:TPU:0, one launch (start us, length us, event | category | flops | bytes accessed | tf_op | source)
XLA Modules:
  0.0 114.4 jit_solution(6580493711377749637)
XLA Ops:
  0.6 5.7 %dispatch.1 = (bf16[1024,1024]{1,0:T(8,128)(2,1)}, s32[1,512]{1,0:T(1,128)}) custom-call(bf16[512,1024]{1,0:T(8,128)(2,1)} %tok_ref.3, s32[1,512]{1,0:T(1,128)} %bitcast.16, f32[1,1024]{1,0:T(1,128)} %bitcast.15), custom_call_target="tpu_custom_call" | custom-call | flops 1073741824 | bytes 4194304 | tf_op jit(solution)/shard_map/dispatch/pallas_call | solution.py:60
  6.3 41.1 %all_to_all.10 = bf16[128,8,1024]{2,1,0:T(8,128)(2,1)} all-to-all(bf16[128,8,1024]{2,1,0:T(8,128)(2,1)} %bitcast.12), channel_id=1, replica_groups=mesh['row_0'=4,'row_1'=2,'col_0'=4,'col_1'=4] {'row_0','row_1','col_0','..., dimensions={0} | all-to-all | bytes 4194304 | tf_op jit(solution)/shard_map/all_to_all | solution.py:195
  47.4 26.2 %expert.1 = (bf16[1024,1024]{1,0:T(8,128)(2,1)}, s32[1]{0:T(128)}) custom-call(bf16[1024,1024]{1,0:T(8,128)(2,1)} %bitcast.11, bf16[1024,4096]{1,0:T(8,128)(2,1)} %bitcast.13, bf16[4096,1024]{1,0:T(8,128)(2,1)} %bitcast.14), custom_call_target="tpu_custom_call" | custom-call | flops 17179869184 | bytes 20971520 | tf_op jit(solution)/shard_map/expert/pallas_call | solution.py:141
  73.6 4.7 %all-to-all-start.1 = ((bf16[128,8,1024]{2,1,0:T(8,128)(2,1)}), bf16[128,8,1024]{2,1,0:T(8,128)(2,1)S(1)}, u32[]{:S(2)}, u32[]{:S(2)}) async-start(bf16[128,8,1024]{2,1,0:T(8,128)(2,1)} %bitcast.10), calls=%async_computation.1 | async-start | bytes 4194304 | tf_op jit(solution)/shard_map/all_to_all | solution.py:195
  78.2 2.1 %prepare.1 = (bf16[512,1024]{1,0:T(8,128)(2,1)}, f32[512,128]{1,0:T(8,128)}) custom-call(s32[1,512]{1,0:T(1,128)} %get-tuple-element.8.placed_ref, f32[1,512]{1,0:T(1,128)} %bitcast.17), custom_call_target="tpu_custom_call" | custom-call | flops 2097152 | bytes 1048576 | tf_op jit(solution)/shard_map/prepare/pallas_call | solution.py:99
  80.3 27.7 %all-to-all-done.1 = bf16[128,8,1024]{2,1,0:T(8,128)(2,1)S(1)} async-done(((bf16[128,8,1024]{2,1,0:T(8,128)(2,1)}), bf16[128,8,1024]{2,1,0:T(8,128)(2,1)S(1)}, u32[]{:S(2)}, u32[]{:S(2)}) %all-to-all-start.1) | async-done | bytes 2097184 | tf_op jit(solution)/shard_map/all_to_all | solution.py:195
  108.0 0.0 copy-start
  108.0 1.3 %copy-done = bf16[128,8,1024]{2,1,0:T(8,128)(2,1)} copy-done((bf16[128,8,1024]{2,1,0:T(8,128)(2,1)}, bf16[128,8,1024]{2,1,0:T(8,128)(2,1)S(1)}, u32[]{:S(2)}) %copy-start) | copy-done | bytes 2097176
  109.4 5.0 %combine.1 = bf16[512,1024]{1,0:T(8,128)(2,1)} custom-call(bf16[512,1024]{1,0:T(8,128)(2,1)} %get-tuple-element.9.table_ref, bf16[1024,1024]{1,0:T(8,128)(2,1)} %bitcast.9, f32[512,128]{1,0:T(8,128)} %get-tuple-element.12.gates_ref, bf16[512,1024]{1,0:T(8,128)(2,1)} %tok_ref.3), custom_call_target="tpu_custom_call" | custom-call | flops 1073741824 | bytes 4194304 | tf_op jit(solution)/shard_map/combine/pallas_call | solution.py:175
Async XLA Ops:
  73.6 34.4 %all-to-all-start.1 = ((bf16[128,8,1024]{2,1,0:T(8,128)(2,1)}), bf16[128,8,1024]{2,1,0:T(8,128)(2,1)S(1)}, u32[]{:S(2)}, u32[]{:S(2)}) async-start(bf16[128,8,1024]{2,1,0:T(8,128)(2,1)} %bitcast.10), calls=%async_computation.1 | async-start | bytes 4194304 | tf_op jit(solution)/shard_map/all_to_all | solution.py:195
  108.0 1.3 %copy-start = (bf16[128,8,1024]{2,1,0:T(8,128)(2,1)}, bf16[128,8,1024]{2,1,0:T(8,128)(2,1)S(1)}, u32[]{:S(2)}) copy-start(bf16[128,8,1024]{2,1,0:T(8,128)(2,1)S(1)} %all-to-all-done.1) | copy-start | bytes 6291460

commit v3 on v2

v3 whole, which is shorter than its diff:
```python
import jax
import jax.numpy as jnp
from jax import lax
from jax.experimental import pallas as pl
from jax.experimental.pallas import tpu as pltpu
from jax.sharding import Mesh
from jax.sharding import PartitionSpec as P

ROW_COL = ("row_0", "row_1", "col_0", "col_1")
EMPTY = 32768.0
MARKED = 128
DISPATCH_COLS = 256
HIDDEN_COLS = 1024
ANSWER_COLS = 512
COMBINE_COLS = 512
VMEM_LIMIT = 50 << 20

HBM = pl.BlockSpec(memory_space=pltpu.HBM)
VMEM = pl.BlockSpec(memory_space=pltpu.VMEM)
SMEM = pl.BlockSpec(memory_space=pltpu.SMEM)


def one_hot(match):
    return jnp.where(match, 1.0, 0.0).astype(jnp.bfloat16)


def columns(block, size):
    start = block * size
    return pl.ds(start if isinstance(block, int) else pl.multiple_of(start, size), size)


def dispatch_kernel(
    tok_hbm, ids_hbm, gain_hbm, out_hbm, placed_ref, tok_ref, ids_ref, gain_ref, sent_ref, in_sem, out_sem
):
    count, width = tok_ref.shape
    blocks, slots, cols = sent_ref.shape
    experts = 128
    capacity = slots // experts
    ids_copy = pltpu.make_async_copy(ids_hbm, ids_ref, in_sem.at[0])
    tok_copy = pltpu.make_async_copy(tok_hbm, tok_ref, in_sem.at[1])
    gain_copy = pltpu.make_async_copy(gain_hbm, gain_ref, in_sem.at[2])
    ids_copy.start()
    tok_copy.start()
    gain_copy.start()
    before = lax.broadcasted_iota(jnp.int32, (count, count), 0) < lax.broadcasted_iota(
        jnp.int32, (count, count), 1
    )
    ids_copy.wait()
    ids = ids_ref[...]
    match = lax.broadcasted_iota(jnp.int32, (experts, count), 0) == ids
    earlier = jnp.dot(one_hot(match), one_hot(before), preferred_element_type=jnp.float32)
    within = jnp.sum(jnp.where(match, earlier, 0.0), axis=0, keepdims=True)
    placed = ids * capacity + within.astype(jnp.int32)
    placed_ref[...] = placed
    table = one_hot(lax.broadcasted_iota(jnp.int32, (slots, count), 0) == placed)
    filled = jnp.dot(
        table, jnp.ones((count, MARKED), jnp.bfloat16), preferred_element_type=jnp.float32
    )
    tok_copy.wait()
    gain_copy.wait()
    wide = tok_ref[...].astype(jnp.float32)
    scale = lax.rsqrt(jnp.mean(wide * wide, axis=1, keepdims=True) + 1e-06)
    normed = (wide * scale * gain_ref[...]).astype(jnp.bfloat16)
    copies = []
    for block in range(blocks):
        sent = jnp.dot(
            table, normed[:, block * cols : (block + 1) * cols], preferred_element_type=jnp.float32
        )
        if block == 0:
            sent_ref[block, :, :MARKED] = jnp.where(filled > 0.5, sent[:, :MARKED], EMPTY).astype(
                jnp.bfloat16
            )
            sent_ref[block, :, MARKED:] = sent[:, MARKED:].astype(jnp.bfloat16)
        else:
            sent_ref[block] = sent.astype(jnp.bfloat16)
        copies.append(
            pltpu.make_async_copy(
                sent_ref.at[block], out_hbm.at[:, columns(block, cols)], out_sem.at[block]
            )
        )
        copies[-1].start()
    for copy in copies:
        copy.wait()


def dispatch(tokens, ids, gain, slots):
    count, width = tokens.shape
    blocks = width // DISPATCH_COLS
    return pl.pallas_call(
        dispatch_kernel,
        in_specs=[HBM, HBM, HBM],
        out_specs=[HBM, VMEM],
        out_shape=[
            pltpu.HBM((slots, width), jnp.bfloat16),
            jax.ShapeDtypeStruct((1, count), jnp.int32),
        ],
        scratch_shapes=[
            pltpu.VMEM((count, width), jnp.bfloat16),
            pltpu.VMEM((1, count), jnp.int32),
            pltpu.VMEM((1, width), jnp.float32),
            pltpu.VMEM((blocks, slots, DISPATCH_COLS), jnp.bfloat16),
            pltpu.SemaphoreType.DMA((3,)),
            pltpu.SemaphoreType.DMA((blocks,)),
        ],
        compiler_params=pltpu.CompilerParams(vmem_limit_bytes=VMEM_LIMIT),
        cost_estimate=pl.CostEstimate(
            flops=2 * slots * count * width, bytes_accessed=4 * slots * width, transcendentals=0
        ),
        name="dispatch",
    )(tokens, ids, gain)


def prepare_kernel(placed_ref, gate_ref, table_ref, gates_ref):
    count, slots = table_ref.shape
    lanes = gates_ref.shape[1]
    rows = jnp.broadcast_to(placed_ref[...].astype(jnp.float32), (lanes, count)).T.astype(jnp.int32)
    gates_ref[...] = jnp.broadcast_to(gate_ref[...], (lanes, count)).T
    lane = lax.broadcasted_iota(jnp.int32, (count, lanes), 1)
    for start in range(0, slots, lanes):
        table_ref[:, start : start + lanes] = one_hot(lane + start == rows)


def prepare(placed, gate, slots):
    count = placed.shape[1]
    return pl.pallas_call(
        prepare_kernel,
        out_shape=[
            jax.ShapeDtypeStruct((count, slots), jnp.bfloat16),
            jax.ShapeDtypeStruct((count, 128), jnp.float32),
        ],
        compiler_params=pltpu.CompilerParams(vmem_limit_bytes=16 << 20),
        cost_estimate=pl.CostEstimate(
            flops=4 * slots * count, bytes_accessed=2 * slots * count, transcendentals=0
        ),
        name="prepare",
    )(placed, gate)


def expert_kernel(
    x_ref, first_hbm, second_hbm, out_hbm, routed_ref,
    first_ref, second_ref, hidden_ref, answer_ref, in_sem, out_sem,
):
    hidden_blocks, _, hidden_cols = first_ref.shape
    answer_blocks, _, answer_cols = second_ref.shape

    def first_copy(block):
        return pltpu.make_async_copy(
            first_hbm.at[:, columns(block, hidden_cols)], first_ref.at[block], in_sem.at[0, block]
        )

    def second_copy(block):
        return pltpu.make_async_copy(
            second_hbm.at[:, columns(block, answer_cols)], second_ref.at[block], in_sem.at[1, block]
        )

    def answer_copy(block):
        return pltpu.make_async_copy(
            answer_ref.at[block], out_hbm.at[:, columns(block, answer_cols)], out_sem.at[block]
        )

    for block in range(hidden_blocks):
        first_copy(block).start()
    for block in range(answer_blocks):
        second_copy(block).start()
    kept = jnp.where(x_ref[:, :MARKED].astype(jnp.float32) < 0.5 * EMPTY, 1.0, 0.0)
    routed_ref[0] = jnp.sum(kept).astype(jnp.int32) // MARKED

    @pl.loop(0, hidden_blocks)
    def _(block):
        first_copy(block).wait()
        hidden = jnp.dot(x_ref[...], first_ref[block], preferred_element_type=jnp.float32)
        hidden_ref[:, columns(block, hidden_cols)] = jnp.maximum(hidden, 0.0).astype(jnp.bfloat16)

    @pl.loop(0, answer_blocks)
    def _(block):
        second_copy(block).wait()
        answer = jnp.dot(hidden_ref[...], second_ref[block], preferred_element_type=jnp.float32)
        answer_ref[block] = answer.astype(jnp.bfloat16)
        answer_copy(block).start()

    for block in range(answer_blocks):
        answer_copy(block).wait()


def expert(x, first, second):
    rows, width = x.shape
    ff = first.shape[1]
    hidden_blocks, answer_blocks = ff // HIDDEN_COLS, width // ANSWER_COLS
    return pl.pallas_call(
        expert_kernel,
        in_specs=[VMEM, HBM, HBM],
        out_specs=[HBM, SMEM],
        out_shape=[
            pltpu.HBM((rows, width), jnp.bfloat16),
            jax.ShapeDtypeStruct((1,), jnp.int32),
        ],
        scratch_shapes=[
            pltpu.VMEM((hidden_blocks, width, HIDDEN_COLS), jnp.bfloat16),
            pltpu.VMEM((answer_blocks, ff, ANSWER_COLS), jnp.bfloat16),
            pltpu.VMEM((rows, ff), jnp.bfloat16),
            pltpu.VMEM((answer_blocks, rows, ANSWER_COLS), jnp.bfloat16),
            pltpu.SemaphoreType.DMA((2, max(hidden_blocks, answer_blocks))),
            pltpu.SemaphoreType.DMA((answer_blocks,)),
        ],
        compiler_params=pltpu.CompilerParams(vmem_limit_bytes=VMEM_LIMIT),
        cost_estimate=pl.CostEstimate(
            flops=4 * rows * width * ff, bytes_accessed=4 * width * (ff + rows), transcendentals=0
        ),
        name="expert",
    )(x, first, second)


def combine_kernel(
    table_ref, back_ref, gates_ref, tok_hbm, out_hbm, tok_ref, mixed_ref, tok_sem, out_sem
):
    blocks, _, cols = mixed_ref.shape
    tok_copy = pltpu.make_async_copy(tok_hbm, tok_ref, tok_sem)
    tok_copy.start()
    gates = jnp.concatenate([gates_ref[...]] * (cols // gates_ref.shape[1]), axis=1)
    copies = []
    for block in range(blocks):
        span = slice(block * cols, (block + 1) * cols)
        back = jnp.dot(table_ref[...], back_ref[:, span], preferred_element_type=jnp.float32)
        if block == 0:
            tok_copy.wait()
        mixed = tok_ref[:, span].astype(jnp.float32) + gates * back
        mixed_ref[block] = mixed.astype(jnp.bfloat16)
        copies.append(
            pltpu.make_async_copy(
                mixed_ref.at[block], out_hbm.at[:, columns(block, cols)], out_sem.at[block]
            )
        )
        copies[-1].start()
    for copy in copies:
        copy.wait()


def combine(table, back, gates, tokens):
    count, width = tokens.shape
    slots = back.shape[0]
    blocks = width // COMBINE_COLS
    return pl.pallas_call(
        combine_kernel,
        in_specs=[VMEM, VMEM, VMEM, HBM],
        out_specs=HBM,
        out_shape=jax.ShapeDtypeStruct((count, width), jnp.bfloat16),
        scratch_shapes=[
            pltpu.VMEM((count, width), jnp.bfloat16),
            pltpu.VMEM((blocks, count, COMBINE_COLS), jnp.bfloat16),
            pltpu.SemaphoreType.DMA,
            pltpu.SemaphoreType.DMA((blocks,)),
        ],
        compiler_params=pltpu.CompilerParams(vmem_limit_bytes=16 << 20),
        cost_estimate=pl.CostEstimate(
            flops=2 * slots * count * width, bytes_accessed=4 * slots * width, transcendentals=0
        ),
        name="combine",
    )(table, back, gates, tokens)


def exchange(rows, devices):
    parts = rows.reshape(devices, rows.shape[0] // devices, rows.shape[1])
    parts = lax.all_to_all(parts, ROW_COL, split_axis=0, concat_axis=0, tiled=True)
    return parts.reshape(rows.shape)


def on_device(tokens, expert_ids, gate_prob, norm_gain, weight_in, weight_out):
    tok_rows, width = tokens.shape
    experts = lax.axis_size(ROW_COL)
    slots = 2 * tok_rows
    tokens = pltpu.with_memory_space_constraint(tokens, pltpu.HBM)
    ids = pltpu.with_memory_space_constraint(expert_ids.reshape(1, tok_rows), pltpu.HBM)
    gain = pltpu.with_memory_space_constraint(norm_gain.reshape(1, width), pltpu.HBM)
    outgoing, placed = dispatch(tokens, ids, gain, slots)
    arrived = exchange(outgoing, experts)
    table, gates = prepare(placed, gate_prob.reshape(1, tok_rows), slots)
    answers, routed = expert(arrived, weight_in[0], weight_out[0])
    returned = exchange(answers, experts)
    mixed = combine(table, returned, gates, tokens)
    return (mixed, routed)


def solution(mesh):
    finer = Mesh(mesh.devices.reshape(4, 2, 4, 4), ROW_COL)
    return jax.shard_map(
        on_device,
        mesh=finer,
        in_specs=(
            P(ROW_COL, None),
            P(ROW_COL, None),
            P(ROW_COL),
            P(),
            P(ROW_COL, None, None),
            P(ROW_COL, None, None),
        ),
        out_specs=(P(ROW_COL, None), P(ROW_COL)),
        check_vma=False,
    )
```

time: 115 us -> 105 us (0.913)
  Pallas kernels: 38.9 us -> 29 us
  waiting for transfers between devices: 27.7 us -> 29.5 us
  local copies, waits for them, and re-layouts: 1.34 us -> 0.01 us
    pallas_call x3, Pallas kernels: 36.9 us -> 28.7 us  [the longest x1 21.6 us: expert(): pl.pallas_call(expert_kernel, in_specs=[VMEM, HBM, HBM], out_specs=[HBM,...]
    pallas_call x1, Pallas kernels: 2.06 us -> 0.29 us  [prepare(): pl.pallas_call(prepare_kernel, out_shape=[jax.ShapeDtypeStruct((count, sl...]
    all_to_all x1, waiting for transfers between devices: 27.7 us -> 29.5 us  [exchange(): lax.all_to_all(parts, ROW_COL, split_axis=0, concat_axis=0, tiled=True)]
    unnamed x2, local copies, waits for them, and re-layouts: 1.34 us -> 0.01 us
  transfers between devices with their start and end apart: 1 -> 1, of which waited for: 1 -> 1; matrix products, arithmetic and copies ran while one was open for 0% -> 0% of each run, Pallas kernels for 2% -> 0%
where the time goes in v3:
time: 105 us
  blocking collectives  41 us (39%)
  waiting for transfers between devices  29.5 us (28%)
  Pallas kernels  29 us (28%)
  starting transfers between devices  4.67 us (4%)
    all_to_all x1, blocking collectives, exchange(): lax.all_to_all(parts, ROW_COL, split_axis=0, concat_axis=0, tiled=True)  41 us
    all_to_all x1, waiting for transfers between devices, exchange(): lax.all_to_all(parts, ROW_COL, split_axis=0, concat_axis=0, tiled=True)  29.5 us
    pallas_call x1, Pallas kernels, expert(): pl.pallas_call(expert_kernel, in_specs=[VMEM, HBM, HBM], out_specs=[HBM,...  21.6 us
    all_to_all x1, starting transfers between devices, exchange(): lax.all_to_all(parts, ROW_COL, split_axis=0, concat_axis=0, tiled=True)  4.67 us
    pallas_call x1, Pallas kernels, dispatch(): pl.pallas_call(dispatch_kernel, in_specs=[HBM, HBM, HBM], out_specs=[HBM,...  4.03 us
    pallas_call x1, Pallas kernels, combine(): pl.pallas_call(combine_kernel, in_specs=[VMEM, VMEM, VMEM, HBM], out_spec...  3.01 us
  transfers between devices with their start and end apart: 1, of which 1 were waited for; matrix products, arithmetic and copies ran while one was open for 0% of the time, Pallas kernels for 0%

profile of v3, /device:TPU:0, one launch (start us, length us, event | category | flops | bytes accessed | tf_op | source)
XLA Modules:
  0.0 104.8 jit_solution(2593388500365555908)
XLA Ops:
  0.6 4.0 %dispatch.1 = (bf16[1024,1024]{1,0:T(8,128)(2,1)}, s32[1,512]{1,0:T(1,128)S(1)}) custom-call(bf16[512,1024]{1,0:T(8,128)(2,1)} %tok_hbm.3, s32[1,512]{1,0:T(1,128)} %bitcast.17, f32[1,1024]{1,0:T(1,128)} %bitcast.16), custom_call_target="tpu_custom_call" | custom-call | flops 1073741824 | bytes 4194304 | tf_op jit(solution)/shard_map/dispatch/pallas_call | solution.py:89
  4.7 41.0 %all_to_all.10 = bf16[128,8,1024]{2,1,0:T(8,128)(2,1)S(1)} all-to-all(bf16[128,8,1024]{2,1,0:T(8,128)(2,1)} %bitcast.13), channel_id=1, replica_groups=mesh['row_0'=4,'row_1'=2,'col_0'=4,'col_1'=4] {'row_0','row_1','col_0','..., dimensions={0} | all-to-all | bytes 4194304 | tf_op jit(solution)/shard_map/all_to_all | solution.py:263
  45.6 21.6 %expert.1 = (bf16[1024,1024]{1,0:T(8,128)(2,1)}, s32[1]{0:T(128)}) custom-call(bf16[1024,1024]{1,0:T(8,128)(2,1)S(1)} %bitcast.10, bf16[1024,4096]{1,0:T(8,128)(2,1)} %bitcast.14, bf16[4096,1024]{1,0:T(8,128)(2,1)} %bitcast.15), custom_call_target="tpu_custom_call" | custom-call | flops 17179869184 | bytes 20971520 | tf_op jit(solution)/shard_map/expert/pallas_call | solution.py:189
  67.3 0.0 copy-start
  67.3 4.7 %all-to-all-start.1 = ((bf16[128,8,1024]{2,1,0:T(8,128)(2,1)}), bf16[128,8,1024]{2,1,0:T(8,128)(2,1)S(1)}, u32[]{:S(2)}, u32[]{:S(2)}) async-start(bf16[128,8,1024]{2,1,0:T(8,128)(2,1)} %bitcast.12), calls=%async_computation.1 | async-start | bytes 4194304 | tf_op jit(solution)/shard_map/all_to_all | solution.py:263
  72.0 0.0 copy-done
  72.0 0.3 prepare.1
  72.3 29.5 %all-to-all-done.1 = bf16[128,8,1024]{2,1,0:T(8,128)(2,1)S(1)} async-done(((bf16[128,8,1024]{2,1,0:T(8,128)(2,1)}), bf16[128,8,1024]{2,1,0:T(8,128)(2,1)S(1)}, u32[]{:S(2)}, u32[]{:S(2)}) %all-to-all-start.1) | async-done | bytes 2097184 | tf_op jit(solution)/shard_map/all_to_all | solution.py:263
  101.7 3.0 %combine.1 = bf16[512,1024]{1,0:T(8,128)(2,1)} custom-call(bf16[512,1024]{1,0:T(8,128)(2,1)S(1)} %get-tuple-element.9.table_ref, bf16[1024,1024]{1,0:T(8,128)(2,1)S(1)} %bitcast.9, f32[512,128]{1,0:T(8,128)S(1)} %get-tuple-element.12.gates_ref, bf16[512,1024]{1,0:T(8,128)(2,1)} %tok_hbm.3), custom_call_target="tpu_custom_call" | custom-call | flops 1073741824 | bytes 4194304 | tf_op jit(solution)/shard_map/combine/pallas_call | solution.py:242
Async XLA Ops:
  67.3 4.7 %copy-start = (f32[512]{0:T(512)S(1)}, f32[512]{0:T(512)}, u32[]{:S(2)}) copy-start(f32[512]{0:T(512)} %param.8) | copy-start | bytes 6148
  67.3 34.4 %all-to-all-start.1 = ((bf16[128,8,1024]{2,1,0:T(8,128)(2,1)}), bf16[128,8,1024]{2,1,0:T(8,128)(2,1)S(1)}, u32[]{:S(2)}, u32[]{:S(2)}) async-start(bf16[128,8,1024]{2,1,0:T(8,128)(2,1)} %bitcast.12), calls=%async_computation.1 | async-start | bytes 4194304 | tf_op jit(solution)/shard_map/all_to_all | solution.py:263

commit v4 on v3

v4 whole, which is shorter than its diff:
```python
import jax
import jax.numpy as jnp
from jax import lax
from jax.experimental import pallas as pl
from jax.experimental.pallas import tpu as pltpu
from jax.sharding import Mesh
from jax.sharding import PartitionSpec as P

ROW_COL = ("row_0", "row_1", "col_0", "col_1")
EMPTY = 32768.0
MARKED = 128
DISPATCH_COLS = 256
HEAD_COLS = 512
HIDDEN_COLS = 512
ANSWER_COLS = 512
COMBINE_COLS = 512
VMEM_LIMIT = 44 << 20

HBM = pl.BlockSpec(memory_space=pltpu.HBM)
VMEM = pl.BlockSpec(memory_space=pltpu.VMEM)
SMEM = pl.BlockSpec(memory_space=pltpu.SMEM)


def one_hot(match):
    return jnp.where(match, 1.0, 0.0).astype(jnp.bfloat16)


def columns(block, size, offset=0):
    start = block * size + offset
    return pl.ds(start if isinstance(block, int) else pl.multiple_of(start, 128), size)


def dispatch_kernel(
    tok_hbm, ids_hbm, gain_hbm, first_hbm, out_ref, placed_ref, head_ref,
    tok_ref, ids_ref, gain_ref, in_sem,
):
    count, width = tok_ref.shape
    slots, cols = out_ref.shape[0], DISPATCH_COLS
    experts = 128
    capacity = slots // experts
    ids_copy = pltpu.make_async_copy(ids_hbm, ids_ref, in_sem.at[0])
    tok_copy = pltpu.make_async_copy(tok_hbm, tok_ref, in_sem.at[1])
    gain_copy = pltpu.make_async_copy(gain_hbm, gain_ref, in_sem.at[2])
    ids_copy.start()
    tok_copy.start()
    gain_copy.start()
    head_copy = pltpu.make_async_copy(
        first_hbm.at[:, pl.ds(0, head_ref.shape[1])], head_ref, in_sem.at[3]
    )
    head_copy.start()
    before = lax.broadcasted_iota(jnp.int32, (count, count), 0) < lax.broadcasted_iota(
        jnp.int32, (count, count), 1
    )
    ids_copy.wait()
    ids = ids_ref[...]
    match = lax.broadcasted_iota(jnp.int32, (experts, count), 0) == ids
    earlier = jnp.dot(one_hot(match), one_hot(before), preferred_element_type=jnp.float32)
    within = jnp.sum(jnp.where(match, earlier, 0.0), axis=0, keepdims=True)
    placed = ids * capacity + within.astype(jnp.int32)
    placed_ref[...] = placed
    table = one_hot(lax.broadcasted_iota(jnp.int32, (slots, count), 0) == placed)
    filled = jnp.dot(
        table, jnp.ones((count, MARKED), jnp.bfloat16), preferred_element_type=jnp.float32
    )
    tok_copy.wait()
    gain_copy.wait()
    wide = tok_ref[...].astype(jnp.float32)
    scale = lax.rsqrt(jnp.mean(wide * wide, axis=1, keepdims=True) + 1e-06)
    normed = (wide * scale * gain_ref[...]).astype(jnp.bfloat16)
    for start in range(0, width, cols):
        sent = jnp.dot(
            table, normed[:, start : start + cols], preferred_element_type=jnp.float32
        )
        if start == 0:
            marked = jnp.where(filled > 0.5, sent[:, :MARKED], EMPTY).astype(jnp.bfloat16)
            out_ref[:, :MARKED] = marked
            out_ref[:, MARKED:cols] = sent[:, MARKED:].astype(jnp.bfloat16)
        else:
            out_ref[:, start : start + cols] = sent.astype(jnp.bfloat16)
    head_copy.wait()


def dispatch(tokens, ids, gain, first, slots):
    count, width = tokens.shape
    return pl.pallas_call(
        dispatch_kernel,
        in_specs=[HBM, HBM, HBM, HBM],
        out_specs=[VMEM, VMEM, VMEM],
        out_shape=[
            pltpu.VMEM((slots, width), jnp.bfloat16),
            jax.ShapeDtypeStruct((1, count), jnp.int32),
            pltpu.VMEM((first.shape[0], HEAD_COLS), jnp.bfloat16),
        ],
        scratch_shapes=[
            pltpu.VMEM((count, width), jnp.bfloat16),
            pltpu.VMEM((1, count), jnp.int32),
            pltpu.VMEM((1, width), jnp.float32),
            pltpu.SemaphoreType.DMA((4,)),
        ],
        compiler_params=pltpu.CompilerParams(vmem_limit_bytes=VMEM_LIMIT),
        cost_estimate=pl.CostEstimate(
            flops=2 * slots * count * width, bytes_accessed=4 * slots * width, transcendentals=0
        ),
        name="dispatch",
    )(tokens, ids, gain, first)


def expert_kernel(
    x_ref, head_ref, placed_ref, gate_ref, first_hbm, second_hbm, tok_hbm,
    out_ref, routed_ref, table_ref, gates_ref, tok_ref,
    first_ref, second_ref, hidden_ref, rows_ref, in_sem, tok_sem,
):
    hidden_blocks, _, hidden_cols = first_ref.shape
    answer_blocks, _, answer_cols = second_ref.shape
    head_cols = head_ref.shape[1]

    def first_copy(block):
        return pltpu.make_async_copy(
            first_hbm.at[:, columns(block, hidden_cols, head_cols)],
            first_ref.at[block],
            in_sem.at[0, block],
        )

    def second_copy(block):
        return pltpu.make_async_copy(
            second_hbm.at[:, columns(block, answer_cols)], second_ref.at[block], in_sem.at[1, block]
        )

    tok_copy = pltpu.make_async_copy(tok_hbm, tok_ref, tok_sem)
    for block in range(hidden_blocks):
        first_copy(block).start()
    for block in range(answer_blocks):
        second_copy(block).start()
    tok_copy.start()
    kept = jnp.where(x_ref[:, :MARKED].astype(jnp.float32) < 0.5 * EMPTY, 1.0, 0.0)
    routed_ref[0] = jnp.sum(kept).astype(jnp.int32) // MARKED

    count, lanes = rows_ref.shape
    placed = jnp.broadcast_to(placed_ref[...].astype(jnp.float32), (lanes, count))
    rows_ref[...] = placed.T.astype(jnp.int32)
    gates_ref[...] = jnp.broadcast_to(gate_ref[...], (lanes, count)).T

    def combine_columns(block):
        lane = lax.broadcasted_iota(jnp.int32, (count, lanes), 1) + block * lanes
        table_ref[:, columns(block, lanes)] = one_hot(lane == rows_ref[...])

    combine_columns(hidden_blocks)
    head = jnp.dot(x_ref[...], head_ref[...], preferred_element_type=jnp.float32)
    hidden_ref[:, :head_cols] = jnp.maximum(head, 0.0).astype(jnp.bfloat16)

    @pl.loop(0, hidden_blocks)
    def _(block):
        first_copy(block).wait()
        combine_columns(block)
        hidden = jnp.dot(x_ref[...], first_ref[block], preferred_element_type=jnp.float32)
        hidden_ref[:, columns(block, hidden_cols, head_cols)] = jnp.maximum(hidden, 0.0).astype(
            jnp.bfloat16
        )

    @pl.loop(0, answer_blocks)
    def _(block):
        second_copy(block).wait()
        answer = jnp.dot(hidden_ref[...], second_ref[block], preferred_element_type=jnp.float32)
        out_ref[:, columns(block, answer_cols)] = answer.astype(jnp.bfloat16)

    tok_copy.wait()


def expert(x, head, placed, gate, first, second, tokens):
    rows, width = x.shape
    ff = first.shape[1]
    hidden_blocks, answer_blocks = (ff - HEAD_COLS) // HIDDEN_COLS, width // ANSWER_COLS
    return pl.pallas_call(
        expert_kernel,
        in_specs=[VMEM, VMEM, VMEM, VMEM, HBM, HBM, HBM],
        out_specs=[VMEM, SMEM, VMEM, VMEM, VMEM],
        out_shape=[
            pltpu.VMEM((rows, width), jnp.bfloat16),
            jax.ShapeDtypeStruct((1,), jnp.int32),
            pltpu.VMEM((placed.shape[1], rows), jnp.bfloat16),
            pltpu.VMEM((placed.shape[1], 128), jnp.float32),
            pltpu.VMEM(tokens.shape, jnp.bfloat16),
        ],
        scratch_shapes=[
            pltpu.VMEM((hidden_blocks, width, HIDDEN_COLS), jnp.bfloat16),
            pltpu.VMEM((answer_blocks, ff, ANSWER_COLS), jnp.bfloat16),
            pltpu.VMEM((rows, ff), jnp.bfloat16),
            pltpu.VMEM((placed.shape[1], 128), jnp.int32),
            pltpu.SemaphoreType.DMA((2, max(hidden_blocks, answer_blocks))),
            pltpu.SemaphoreType.DMA,
        ],
        compiler_params=pltpu.CompilerParams(vmem_limit_bytes=VMEM_LIMIT),
        cost_estimate=pl.CostEstimate(
            flops=4 * rows * width * ff, bytes_accessed=4 * width * (ff + rows), transcendentals=0
        ),
        name="expert",
    )(x, head, placed, gate, first, second, tokens)


def combine_kernel(
    table_ref, back_ref, gates_ref, tok_ref, out_hbm, mixed_ref, out_sem
):
    blocks, _, cols = mixed_ref.shape
    gates = jnp.concatenate([gates_ref[...]] * (cols // gates_ref.shape[1]), axis=1)
    copies = []
    for block in range(blocks):
        span = slice(block * cols, (block + 1) * cols)
        back = jnp.dot(table_ref[...], back_ref[:, span], preferred_element_type=jnp.float32)
        mixed = tok_ref[:, span].astype(jnp.float32) + gates * back
        mixed_ref[block] = mixed.astype(jnp.bfloat16)
        copies.append(
            pltpu.make_async_copy(
                mixed_ref.at[block], out_hbm.at[:, columns(block, cols)], out_sem.at[block]
            )
        )
        copies[-1].start()
    for copy in copies:
        copy.wait()


def combine(table, back, gates, tokens):
    count, width = tokens.shape
    slots = back.shape[0]
    blocks = width // COMBINE_COLS
    return pl.pallas_call(
        combine_kernel,
        in_specs=[VMEM, VMEM, VMEM, VMEM],
        out_specs=HBM,
        out_shape=jax.ShapeDtypeStruct((count, width), jnp.bfloat16),
        scratch_shapes=[
            pltpu.VMEM((blocks, count, COMBINE_COLS), jnp.bfloat16),
            pltpu.SemaphoreType.DMA((blocks,)),
        ],
        compiler_params=pltpu.CompilerParams(vmem_limit_bytes=16 << 20),
        cost_estimate=pl.CostEstimate(
            flops=2 * slots * count * width, bytes_accessed=4 * slots * width, transcendentals=0
        ),
        name="combine",
    )(table, back, gates, tokens)


def exchange(rows, devices):
    parts = rows.reshape(devices, rows.shape[0] // devices, rows.shape[1])
    parts = lax.all_to_all(parts, ROW_COL, split_axis=0, concat_axis=0, tiled=True)
    return parts.reshape(rows.shape)


def on_device(tokens, expert_ids, gate_prob, norm_gain, weight_in, weight_out):
    tok_rows, width = tokens.shape
    experts = lax.axis_size(ROW_COL)
    slots = 2 * tok_rows
    tokens = pltpu.with_memory_space_constraint(tokens, pltpu.HBM)
    ids = pltpu.with_memory_space_constraint(expert_ids.reshape(1, tok_rows), pltpu.HBM)
    gain = pltpu.with_memory_space_constraint(norm_gain.reshape(1, width), pltpu.HBM)
    first = pltpu.with_memory_space_constraint(weight_in[0], pltpu.HBM)
    second = pltpu.with_memory_space_constraint(weight_out[0], pltpu.HBM)
    outgoing, placed, head = dispatch(tokens, ids, gain, first, slots)
    arrived = pltpu.with_memory_space_constraint(exchange(outgoing, experts), pltpu.VMEM)
    gate = gate_prob.reshape(1, tok_rows)
    answers, routed, table, gates, held = expert(
        arrived, head, placed, gate, first, second, tokens
    )
    returned = pltpu.with_memory_space_constraint(exchange(answers, experts), pltpu.VMEM)
    mixed = combine(table, returned, gates, held)
    return (mixed, routed)


def solution(mesh):
    finer = Mesh(mesh.devices.reshape(4, 2, 4, 4), ROW_COL)
    return jax.shard_map(
        on_device,
        mesh=finer,
        in_specs=(
            P(ROW_COL, None),
            P(ROW_COL, None),
            P(ROW_COL),
            P(),
            P(ROW_COL, None, None),
            P(ROW_COL, None, None),
        ),
        out_specs=(P(ROW_COL, None), P(ROW_COL)),
        check_vma=False,
    )
```

time: 105 us -> 101 us (0.962)
  blocking collectives: 41 us -> 74.9 us
  waiting for transfers between devices: 29.5 us -> 0 us
  starting transfers between devices: 4.67 us -> 0 us
  Pallas kernels: 29 us -> 25.4 us
    all_to_all x1 -> x2, blocking collectives: 41 us -> 74.9 us  [exchange(): lax.all_to_all(parts, ROW_COL, split_axis=0, concat_axis=0, tiled=True)]
    all_to_all x1 -> x0, waiting for transfers between devices: 29.5 us -> none  [exchange(): lax.all_to_all(parts, ROW_COL, split_axis=0, concat_axis=0, tiled=True)]
    all_to_all x1 -> x0, starting transfers between devices: 4.67 us -> none  [exchange(): lax.all_to_all(parts, ROW_COL, split_axis=0, concat_axis=0, tiled=True)]
    pallas_call x4 -> x3, Pallas kernels: 29 us -> 25.4 us  [the longest x1 20.4 us: expert(): pl.pallas_call(expert_kernel, in_specs=[VMEM, VMEM, VMEM, VMEM, HBM, HBM,...]
  transfers between devices with their start and end apart: 1 -> 0, of which waited for: 1 -> 0; matrix products, arithmetic and copies ran while one was open for 0% -> 0% of each run, Pallas kernels for 0% -> 0%
where the time goes in v4:
time: 101 us
  blocking collectives  74.9 us (74%)
  Pallas kernels  25.4 us (25%)
    all_to_all x2, blocking collectives, exchange(): lax.all_to_all(parts, ROW_COL, split_axis=0, concat_axis=0, tiled=True)  74.9 us
    pallas_call x1, Pallas kernels, expert(): pl.pallas_call(expert_kernel, in_specs=[VMEM, VMEM, VMEM, VMEM, HBM, HBM,...  20.4 us
    pallas_call x1, Pallas kernels, dispatch(): pl.pallas_call(dispatch_kernel, in_specs=[HBM, HBM, HBM, HBM], out_specs=...  2.91 us
    pallas_call x1, Pallas kernels, combine(): pl.pallas_call(combine_kernel, in_specs=[VMEM, VMEM, VMEM, VMEM], out_spe...  2.09 us

profile of v4, /device:TPU:0, one launch (start us, length us, event | category | flops | bytes accessed | tf_op | source)
XLA Modules:
  0.0 101.0 jit_solution(1799985056863092049)
XLA Ops:
  0.6 2.9 %dispatch.1 = (bf16[1024,1024]{1,0:T(8,128)(2,1)S(1)}, s32[1,512]{1,0:T(1,128)S(1)}, bf16[1024,512]{1,0:T(8,128)(2,1)S(1)}) custom-call(bf16[512,1024]{1,0:T(8,128)(2,1)} %tok_hbm.3, s32[1,512]{1,0:T(1,128)} %bitcast.17, f32[1,1024]{1,0:T(1,128)} %bitcast.16, bf16[1024,4096]{1,0:T(8,128)(2,1)} %bitcast.14), custom_call_target="tpu_custom_call" | custom-call | flops 1073741824 | bytes 4194304 | tf_op jit(solution)/shard_map/dispatch/pallas_call | solution.py:85
  3.5 0.0 copy-start
  3.6 40.8 %all_to_all.10 = bf16[128,8,1024]{2,1,0:T(8,128)(2,1)S(1)} all-to-all(bf16[128,8,1024]{2,1,0:T(8,128)(2,1)S(1)} %bitcast.12), channel_id=1, replica_groups=mesh['row_0'=4,'row_1'=2,'col_0'=4,'col_1'=4] {'row_0','row_1','col_0','..., dimensions={0} | all-to-all | bytes 4194304 | tf_op jit(solution)/shard_map/all_to_all | solution.py:244
  44.3 0.0 copy-done
  44.3 20.4 %expert.1 = (bf16[1024,1024]{1,0:T(8,128)(2,1)S(1)}, s32[1]{0:T(128)}, bf16[512,1024]{1,0:T(8,128)(2,1)S(1)}, f32[512,128]{1,0:T(8,128)S(1)}, bf16[512,1024]{1,0:T(8,128)(2,1)S(1)}) custom-call(bf16[1024,1024]{1,0:T(8,128)(2,1)S(1)} %bitcast.10, bf16[1024,512]{1,0:T(8,128)(2,1)S(1)} %get-tuple-element.11.head_ref, ...), custom_call_target="tpu_custom_call" | custom-call | flops 17179869184 | bytes 20971520 | tf_op jit(solution)/shard_map/expert/pallas_call | solution.py:173
  64.7 34.2 %all_to_all.11 = bf16[128,8,1024]{2,1,0:T(8,128)(2,1)S(1)} all-to-all(bf16[128,8,1024]{2,1,0:T(8,128)(2,1)S(1)} %bitcast.11), channel_id=1, replica_groups=mesh['row_0'=4,'row_1'=2,'col_0'=4,'col_1'=4] {'row_0','row_1','col_0','..., dimensions={0} | all-to-all | bytes 4194304 | tf_op jit(solution)/shard_map/all_to_all | solution.py:244
  98.9 2.1 %combine.1 = bf16[512,1024]{1,0:T(8,128)(2,1)} custom-call(bf16[512,1024]{1,0:T(8,128)(2,1)S(1)} %get-tuple-element.13.table_ref, bf16[1024,1024]{1,0:T(8,128)(2,1)S(1)} %bitcast.9, f32[512,128]{1,0:T(8,128)S(1)} %get-tuple-element.15.gates_ref, bf16[512,1024]{1,0:T(8,128)(2,1)S(1)} %get-tuple-element.16.tok_ref), custom_call_target="tpu_custom_call" | custom-call | flops 1073741824 | bytes 4194304 | tf_op jit(solution)/shard_map/combine/pallas_call | solution.py:225
Async XLA Ops:
  3.5 40.8 %copy-start = (f32[512]{0:T(512)S(1)}, f32[512]{0:T(512)}, u32[]{:S(2)}) copy-start(f32[512]{0:T(512)} %param.8) | copy-start | bytes 6148

commit v5 on v4

--- a/solution.py
+++ b/solution.py
@@ -144,14 +144,12 @@
         lane = lax.broadcasted_iota(jnp.int32, (count, lanes), 1) + block * lanes
         table_ref[:, columns(block, lanes)] = one_hot(lane == rows_ref[...])
 
-    combine_columns(hidden_blocks)
     head = jnp.dot(x_ref[...], head_ref[...], preferred_element_type=jnp.float32)
     hidden_ref[:, :head_cols] = jnp.maximum(head, 0.0).astype(jnp.bfloat16)
 
     @pl.loop(0, hidden_blocks)
     def _(block):
         first_copy(block).wait()
-        combine_columns(block)
         hidden = jnp.dot(x_ref[...], first_ref[block], preferred_element_type=jnp.float32)
         hidden_ref[:, columns(block, hidden_cols, head_cols)] = jnp.maximum(hidden, 0.0).astype(
             jnp.bfloat16
@@ -160,6 +158,9 @@
     @pl.loop(0, answer_blocks)
     def _(block):
         second_copy(block).wait()
+        steps = table_ref.shape[1] // lanes // answer_blocks
+        for step in range(steps):
+            combine_columns(block * steps + step)
         answer = jnp.dot(hidden_ref[...], second_ref[block], preferred_element_type=jnp.float32)
         out_ref[:, columns(block, answer_cols)] = answer.astype(jnp.bfloat16)
 

time: 101 us -> 101 us (level)
  no operation moved by 1% of the time
where the time goes in v5:
time: 101 us
  blocking collectives  74.9 us (74%)
  Pallas kernels  25.1 us (25%)
    all_to_all x2, blocking collectives, exchange(): lax.all_to_all(parts, ROW_COL, split_axis=0, concat_axis=0, tiled=True)  74.9 us
    pallas_call x1, Pallas kernels, expert(): pl.pallas_call(expert_kernel, in_specs=[VMEM, VMEM, VMEM, VMEM, HBM, HBM,...  20.1 us
    pallas_call x1, Pallas kernels, dispatch(): pl.pallas_call(dispatch_kernel, in_specs=[HBM, HBM, HBM, HBM], out_specs=...  2.91 us
    pallas_call x1, Pallas kernels, combine(): pl.pallas_call(combine_kernel, in_specs=[VMEM, VMEM, VMEM, VMEM], out_spe...  2.09 us

profile of v5, /device:TPU:0, one launch (start us, length us, event | category | flops | bytes accessed | tf_op | source)
XLA Modules:
  0.0 100.7 jit_solution(7933536033442469639)
XLA Ops:
  0.6 2.9 %dispatch.1 = (bf16[1024,1024]{1,0:T(8,128)(2,1)S(1)}, s32[1,512]{1,0:T(1,128)S(1)}, bf16[1024,512]{1,0:T(8,128)(2,1)S(1)}) custom-call(bf16[512,1024]{1,0:T(8,128)(2,1)} %tok_hbm.3, s32[1,512]{1,0:T(1,128)} %bitcast.17, f32[1,1024]{1,0:T(1,128)} %bitcast.16, bf16[1024,4096]{1,0:T(8,128)(2,1)} %bitcast.14), custom_call_target="tpu_custom_call" | custom-call | flops 1073741824 | bytes 4194304 | tf_op jit(solution)/shard_map/dispatch/pallas_call | solution.py:85
  3.5 0.0 copy-start
  3.6 40.8 %all_to_all.10 = bf16[128,8,1024]{2,1,0:T(8,128)(2,1)S(1)} all-to-all(bf16[128,8,1024]{2,1,0:T(8,128)(2,1)S(1)} %bitcast.12), channel_id=1, replica_groups=mesh['row_0'=4,'row_1'=2,'col_0'=4,'col_1'=4] {'row_0','row_1','col_0','..., dimensions={0} | all-to-all | bytes 4194304 | tf_op jit(solution)/shard_map/all_to_all | solution.py:245
  44.3 0.0 copy-done
  44.3 20.1 %expert.1 = (bf16[1024,1024]{1,0:T(8,128)(2,1)S(1)}, s32[1]{0:T(128)}, bf16[512,1024]{1,0:T(8,128)(2,1)S(1)}, f32[512,128]{1,0:T(8,128)S(1)}, bf16[512,1024]{1,0:T(8,128)(2,1)S(1)}) custom-call(bf16[1024,1024]{1,0:T(8,128)(2,1)S(1)} %bitcast.10, bf16[1024,512]{1,0:T(8,128)(2,1)S(1)} %get-tuple-element.11.head_ref, ...), custom_call_target="tpu_custom_call" | custom-call | flops 17179869184 | bytes 20971520 | tf_op jit(solution)/shard_map/expert/pallas_call | solution.py:174
  64.4 34.2 %all_to_all.11 = bf16[128,8,1024]{2,1,0:T(8,128)(2,1)S(1)} all-to-all(bf16[128,8,1024]{2,1,0:T(8,128)(2,1)S(1)} %bitcast.11), channel_id=1, replica_groups=mesh['row_0'=4,'row_1'=2,'col_0'=4,'col_1'=4] {'row_0','row_1','col_0','..., dimensions={0} | all-to-all | bytes 4194304 | tf_op jit(solution)/shard_map/all_to_all | solution.py:245
  98.6 2.1 %combine.1 = bf16[512,1024]{1,0:T(8,128)(2,1)} custom-call(bf16[512,1024]{1,0:T(8,128)(2,1)S(1)} %get-tuple-element.13.table_ref, bf16[1024,1024]{1,0:T(8,128)(2,1)S(1)} %bitcast.9, f32[512,128]{1,0:T(8,128)S(1)} %get-tuple-element.15.gates_ref, bf16[512,1024]{1,0:T(8,128)(2,1)S(1)} %get-tuple-element.16.tok_ref), custom_call_target="tpu_custom_call" | custom-call | flops 1073741824 | bytes 4194304 | tf_op jit(solution)/shard_map/combine/pallas_call | solution.py:226
Async XLA Ops:
  3.5 40.8 %copy-start = (f32[512]{0:T(512)S(1)}, f32[512]{0:T(512)}, u32[]{:S(2)}) copy-start(f32[512]{0:T(512)} %param.8) | copy-start | bytes 6148

commit v6 on v5

--- a/solution.py
+++ b/solution.py
@@ -59,9 +59,11 @@
     placed = ids * capacity + within.astype(jnp.int32)
     placed_ref[...] = placed
     table = one_hot(lax.broadcasted_iota(jnp.int32, (slots, count), 0) == placed)
-    filled = jnp.dot(
-        table, jnp.ones((count, MARKED), jnp.bfloat16), preferred_element_type=jnp.float32
-    )
+    taken = jnp.dot(
+        one_hot(match), jnp.ones((count, MARKED), jnp.bfloat16), preferred_element_type=jnp.float32
+    )
+    slot = lax.broadcasted_iota(jnp.int32, (experts, capacity, MARKED), 1).astype(jnp.float32)
+    filled = jnp.where(slot < taken[:, None, :], 1.0, 0.0).reshape(slots, MARKED)
     tok_copy.wait()
     gain_copy.wait()
     wide = tok_ref[...].astype(jnp.float32)

time: 101 us -> 101 us (level)
  no operation moved by 1% of the time
where the time goes in v6:
time: 101 us
  blocking collectives  74.9 us (74%)
  Pallas kernels  25 us (25%)
    all_to_all x2, blocking collectives, exchange(): lax.all_to_all(parts, ROW_COL, split_axis=0, concat_axis=0, tiled=True)  74.9 us
    pallas_call x1, Pallas kernels, expert(): pl.pallas_call(expert_kernel, in_specs=[VMEM, VMEM, VMEM, VMEM, HBM, HBM,...  20.1 us
    pallas_call x1, Pallas kernels, dispatch(): pl.pallas_call(dispatch_kernel, in_specs=[HBM, HBM, HBM, HBM], out_specs=...  2.86 us
    pallas_call x1, Pallas kernels, combine(): pl.pallas_call(combine_kernel, in_specs=[VMEM, VMEM, VMEM, VMEM], out_spe...  2.09 us

profile of v6, /device:TPU:0, one launch (start us, length us, event | category | flops | bytes accessed | tf_op | source)
XLA Modules:
  0.0 100.7 jit_solution(13254885444009248498)
XLA Ops:
  0.6 2.9 %dispatch.1 = (bf16[1024,1024]{1,0:T(8,128)(2,1)S(1)}, s32[1,512]{1,0:T(1,128)S(1)}, bf16[1024,512]{1,0:T(8,128)(2,1)S(1)}) custom-call(bf16[512,1024]{1,0:T(8,128)(2,1)} %tok_hbm.3, s32[1,512]{1,0:T(1,128)} %bitcast.17, f32[1,1024]{1,0:T(1,128)} %bitcast.16, bf16[1024,4096]{1,0:T(8,128)(2,1)} %bitcast.14), custom_call_target="tpu_custom_call" | custom-call | flops 1073741824 | bytes 4194304 | tf_op jit(solution)/shard_map/dispatch/pallas_call | solution.py:87
  3.5 0.0 copy-start
  3.5 40.8 %all_to_all.10 = bf16[128,8,1024]{2,1,0:T(8,128)(2,1)S(1)} all-to-all(bf16[128,8,1024]{2,1,0:T(8,128)(2,1)S(1)} %bitcast.12), channel_id=1, replica_groups=mesh['row_0'=4,'row_1'=2,'col_0'=4,'col_1'=4] {'row_0','row_1','col_0','..., dimensions={0} | all-to-all | bytes 4194304 | tf_op jit(solution)/shard_map/all_to_all | solution.py:247
  44.3 0.0 copy-done
  44.3 20.1 %expert.1 = (bf16[1024,1024]{1,0:T(8,128)(2,1)S(1)}, s32[1]{0:T(128)}, bf16[512,1024]{1,0:T(8,128)(2,1)S(1)}, f32[512,128]{1,0:T(8,128)S(1)}, bf16[512,1024]{1,0:T(8,128)(2,1)S(1)}) custom-call(bf16[1024,1024]{1,0:T(8,128)(2,1)S(1)} %bitcast.10, bf16[1024,512]{1,0:T(8,128)(2,1)S(1)} %get-tuple-element.11.head_ref, ...), custom_call_target="tpu_custom_call" | custom-call | flops 17179869184 | bytes 20971520 | tf_op jit(solution)/shard_map/expert/pallas_call | solution.py:176
  64.4 34.2 %all_to_all.11 = bf16[128,8,1024]{2,1,0:T(8,128)(2,1)S(1)} all-to-all(bf16[128,8,1024]{2,1,0:T(8,128)(2,1)S(1)} %bitcast.11), channel_id=1, replica_groups=mesh['row_0'=4,'row_1'=2,'col_0'=4,'col_1'=4] {'row_0','row_1','col_0','..., dimensions={0} | all-to-all | bytes 4194304 | tf_op jit(solution)/shard_map/all_to_all | solution.py:247
  98.6 2.1 %combine.1 = bf16[512,1024]{1,0:T(8,128)(2,1)} custom-call(bf16[512,1024]{1,0:T(8,128)(2,1)S(1)} %get-tuple-element.13.table_ref, bf16[1024,1024]{1,0:T(8,128)(2,1)S(1)} %bitcast.9, f32[512,128]{1,0:T(8,128)S(1)} %get-tuple-element.15.gates_ref, bf16[512,1024]{1,0:T(8,128)(2,1)S(1)} %get-tuple-element.16.tok_ref), custom_call_target="tpu_custom_call" | custom-call | flops 1073741824 | bytes 4194304 | tf_op jit(solution)/shard_map/combine/pallas_call | solution.py:228
Async XLA Ops:
  3.5 40.8 %copy-start = (f32[512]{0:T(512)S(1)}, f32[512]{0:T(512)}, u32[]{:S(2)}) copy-start(f32[512]{0:T(512)} %param.8) | copy-start | bytes 6148
